TPU v7x, 256 devices: a whole 4x4x8 slice. The times are simulated.
256 devices in a mesh: dp: 256 (over y, z, x, core).
Axes of the slice: x: 4, y: 4, z: 8, core: 2. Of those that a mesh axis runs over, the one named last changes fastest.
Arguments:
- master: float32 [524288], P('dp'), may hold values from -6 to 6
- gradients: float32 [524288], P('dp'), may hold values from -6 to 6
- first_moment: float32 [524288], P('dp'), may hold values from -4 to 4
- second_moment: float32 [524288], P('dp'), may hold values from 0.01 to 1
- segment_ids: int32 [524288], P('dp'), may hold values from 0 to 511, as said below
- decay_mask: int32 [512], replicated, may hold values 0 or 1
Outputs:
- new_master: float32 [524288], P('dp')
- new_first: float32 [524288], P('dp')
- new_second: float32 [524288], P('dp')
- scaled_step: float32 [524288], P('dp')
- model_weights: bfloat16 [524288], replicated
Inputs may be any that keep to these rules, and one draw needn't show every extreme that they name: segment_ids never falls along the flat vector; each tensor 0 to 511 owns one contiguous run of 256 to 16384 elements, and one tensor has exactly 16384. `decay_mask`: each entry is 0 or 1.
All inputs are finite; a program needn't handle non-finite values.
Results may differ from a plain program's by a relative error of at most 0.0004.
Values may be sent and summed in bfloat16 or wider, within the bound.
A program may use at most 64 MiB of HBM per device.

v0:
```python
import functools
import math
import jax
import jax.numpy as jnp
from jax import lax
from jax.sharding import Mesh
from jax.sharding import PartitionSpec as P

SEG_DEV = 2
STEP = 20
DP = ("dp_0", "dp_1", "dp_2", "dp_3")
first_decay = 0.9
second_decay = 0.999
epsilon = 1e-06
weight_decay = 0.01
learn_rate = 0.006


def one_axis_at_a_time(value, axes):
    return functools.reduce(lax.psum, axes, value)


def adam_direction(master, gradients, first_moment, second_moment, decay):
    new_first = first_decay * first_moment + (1.0 - first_decay) * gradients
    new_second = second_decay * second_moment + (1.0 - second_decay) * gradients * gradients
    hat_first = new_first / (1.0 - first_decay**STEP)
    hat_second = new_second / (1.0 - second_decay**STEP)
    direction = hat_first / (jnp.sqrt(hat_second) + epsilon) + weight_decay * decay * master
    return (new_first, new_second, direction)


def trust_ratio(weight_sq, step_sq):
    weight_norm = jnp.sqrt(weight_sq)
    step_norm = jnp.sqrt(step_sq)
    usable = (weight_norm > 0.0) & (step_norm > 0.0)
    return jnp.where(usable, weight_norm / jnp.where(usable, step_norm, 1.0), 1.0)


def block_rows(length):
    return math.gcd(length, 1024)


def one_hot_block(ids, width):
    columns = lax.broadcasted_iota(jnp.int32, (ids.shape[0], width), 1)
    return (ids[:, None] == columns).astype(jnp.float32)


def spread(table, ids, width):
    length = ids.shape[0]
    rows = block_rows(length)
    blocks = ids.reshape(length // rows, rows)

    def one_block(block_ids):
        return jnp.dot(one_hot_block(block_ids, width), table, precision=lax.Precision.HIGHEST)

    return lax.map(one_block, blocks).reshape(length, table.shape[1])


def collect(values, ids, width):
    length = ids.shape[0]
    rows = block_rows(length)
    blocks = ids.reshape(length // rows, rows)
    value_blocks = values.reshape(length // rows, rows, values.shape[1])

    def add_block(total, pair):
        block_ids, block_values = pair
        term = lax.dot_general(
            one_hot_block(block_ids, width),
            block_values,
            (((0,), (0,)), ((), ())),
            precision=lax.Precision.HIGHEST,
        )
        return (total + term, None)

    start = jnp.zeros((width, values.shape[1]), jnp.float32)
    total, unused = lax.scan(add_block, start, (blocks, value_blocks))
    return total


def to_global(partial_value, first_id, tensors, width):
    holder = jnp.zeros((tensors + width, partial_value.shape[1]), jnp.float32)
    placed = lax.dynamic_update_slice_in_dim(holder, partial_value, first_id, 0)
    return placed[:tensors]


def to_local(table, first_id, width, filler):
    padded = jnp.concatenate([table, jnp.full((width,), filler, jnp.float32)])
    return lax.dynamic_slice_in_dim(padded, first_id, width)


def shards(master, gradients, first_moment, second_moment, segment_ids, decay_mask):
    tensors = decay_mask.shape[0]
    width = 4 * SEG_DEV + 2
    first_id = segment_ids[0].astype(jnp.int32)
    local_ids = (segment_ids - first_id).astype(jnp.int32)
    local_mask = to_local(decay_mask.astype(jnp.float32), first_id, width, 0.0)
    decay = spread(local_mask[:, None], local_ids, width)[:, 0]
    weight_square = master * master
    new_first, new_second, direction = adam_direction(
        master, gradients, first_moment, second_moment, decay
    )
    stacked = jnp.stack([weight_square, direction * direction], axis=1)
    packed_partial = to_global(collect(stacked, local_ids, width), first_id, tensors, width)
    totals = one_axis_at_a_time(packed_partial, DP)
    ratios = to_local(trust_ratio(totals[:, 0], totals[:, 1]), first_id, width, 1.0)
    per_element = spread(ratios[:, None], local_ids, width)[:, 0]
    scaled_step = per_element * direction
    new_master = master - learn_rate * scaled_step
    model_weights = lax.all_gather(new_master.astype(jnp.bfloat16), DP, axis=0, tiled=True)
    return (new_master, new_first, new_second, scaled_step, model_weights)


def solution(mesh):
    torus = Mesh(mesh.devices.reshape(4, 8, 4, 2), ("dp_0", "dp_1", "dp_2", "dp_3"))
    return jax.shard_map(
        shards,
        mesh=torus,
        in_specs=(P(DP), P(DP), P(DP), P(DP), P(DP), P()),
        out_specs=(P(DP), P(DP), P(DP), P(DP), P()),
        check_vma=False,
    )
```

profile of v0, /device:TPU:1, one launch (start us, length us, event | category | flops | bytes accessed | tf_op | source)
XLA Modules:
  0.0 167.1 jit_solution(12047578045685534841)
XLA Ops:
  7.2 0.0 copy-start.4
  7.2 0.0 all-gather.2.cloned.1.call-start
  7.2 1.2 slice.12
  9.1 0.0 copy-done.4
  9.1 0.0 copy-start.5
  9.1 0.7 broadcast_subtract_fusion
  10.4 0.0 copy-done.5
  11.1 0.1 fusion.10
  11.2 0.0 copy-start.2
  11.2 0.0 copy-start.3
  11.2 1.0 while.31
  11.2 0.5 fusion.23
  11.7 0.5 fusion.23
  12.2 0.0 copy-start
  12.2 0.0 copy-start.1
  12.2 0.0 copy-done.2
  12.2 0.0 copy-done.3
  12.2 0.7 copy-done
  12.9 0.0 copy-done.1
  12.9 0.6 fusion.13
  13.5 0.8 while.33
  13.6 0.4 convolution_add_fusion.2
  14.0 0.4 convolution_add_fusion.2
  14.4 0.3 dynamic_update_slice.10
  14.7 9.5 %psum.28 = f32[512,2]{0,1:T(2,128)S(1)} all-reduce(f32[512,2]{0,1:T(2,128)S(1)} %slice.16), channel_id=1, replica_groups=mesh['dp_0'=4,'dp_1'=8,'dp_2'=4,'dp_3'=2] {'dp_0'}, use_global_device_ids=true, to_apply=%region_4.5 | all-reduce | flops 1024 | bytes 8192 | tf_op jit(solution)/shard_map/psum | solution.py:20
  24.2 16.2 %psum.29 = f32[512,2]{0,1:T(2,128)S(1)} all-reduce(f32[512,2]{0,1:T(2,128)S(1)} %psum.28), channel_id=1, replica_groups=mesh['dp_0'=4,'dp_1'=8,'dp_2'=4,'dp_3'=2] {'dp_1'}, use_global_device_ids=true, to_apply=%region_5.6 | all-reduce | flops 1024 | bytes 8192 | tf_op jit(solution)/shard_map/psum | solution.py:20
  40.4 8.5 %psum.30 = f32[512,2]{0,1:T(2,128)S(1)} all-reduce(f32[512,2]{0,1:T(2,128)S(1)} %psum.29), channel_id=1, replica_groups=mesh['dp_0'=4,'dp_1'=8,'dp_2'=4,'dp_3'=2] {'dp_2'}, use_global_device_ids=true, to_apply=%region_6.7 | all-reduce | flops 1024 | bytes 8192 | tf_op jit(solution)/shard_map/psum | solution.py:20
  48.9 10.6 %psum.31 = f32[512,2]{0,1:T(2,128)S(1)} all-reduce(f32[512,2]{0,1:T(2,128)S(1)} %psum.30), channel_id=1, replica_groups=mesh['dp_0'=4,'dp_1'=8,'dp_2'=4,'dp_3'=2] {'dp_3'}, use_global_device_ids=true, to_apply=%region_7.8 | all-reduce | flops 1024 | bytes 8192 | tf_op jit(solution)/shard_map/psum | solution.py:20
  59.5 0.1 fusion.11
  59.6 0.9 while.32
  59.6 0.5 fusion.25
  60.1 0.5 fusion.25
  60.6 0.6 fusion.12
  61.2 0.0 all-gather.2.cloned.1.call-update
  61.2 96.8 %all-gather.2.cloned.1.call-done = bf16[524288]{0:T(1024)(128)(2,1)} async-done(((bf16[2048]{0:T(1024)(128)(2,1)}), bf16[524288]{0:T(1024)(128)(2,1)}) %all-gather.2.cloned.1.call-update) | async-done | bytes 1048592 | tf_op jit(solution)/shard_map/all_gather | solution.py:109
  158.0 2.3 %copy.35 = bf16[524288]{0:T(1024)(128)(2,1)} copy(bf16[524288]{0:T(1024)(128)(2,1)} %all-gather.2.cloned.1.call-done) | data formatting | bytes 2097152
  (17 shorter events, 0.2 us)
Async XLA Ops:
  7.2 1.9 %copy-start.4 = (s32[2048]{0:T(1024)S(1)}, s32[2048]{0:T(1024)}, u32[]{:S(2)}) copy-start(s32[2048]{0:T(1024)} %param.16) | copy-start | bytes 24580
  7.2 150.8 %all-gather.2.cloned.1.call-start = ((), (), s32[]{:S(2)}) async-start(), calls=%async_computation | async-start | bytes 1052672 | tf_op jit(solution)/shard_map/all_gather | solution.py:109
  9.1 1.3 copy-start.5
  11.2 1.0 copy-start.2
  11.2 1.0 copy-start.3
  12.2 0.7 copy-start
  12.2 0.7 copy-start.1
Sparse Core Ops, SparseCore 0:
  61.3 96.5 all-gather.1
where the time goes:
time: 167 us
  waiting for transfers between devices  96.8 us (58%)
  blocking collectives  44.8 us (27%)
  between operations  16.1 us (10%)
  local copies, waits for them, and re-layouts  4.7 us (3%)
  matrix products  2.58 us (2%)
  other arithmetic  1.93 us (1%)
    all_gather x1, waiting for transfers between devices, shards(): lax.all_gather(new_master.astype(jnp.bfloat16), DP, axis=0, tiled=True)  96.8 us
    psum x4, blocking collectives, one_axis_at_a_time(): return functools.reduce(lax.psum, axes, value)  44.8 us
  transfers between devices with their start and end apart: 1, of which 1 were waited for; matrix products, arithmetic and copies ran while one was open for 0% of the time, Pallas kernels for 0%

commit v1 on v0

--- a/solution.py
+++ b/solution.py
@@ -106,7 +106,10 @@
     per_element = spread(ratios[:, None], local_ids, width)[:, 0]
     scaled_step = per_element * direction
     new_master = master - learn_rate * scaled_step
-    model_weights = lax.all_gather(new_master.astype(jnp.bfloat16), DP, axis=0, tiled=True)
+    model_weights = jnp.concatenate(
+        lax.all_to_all(jnp.stack([new_master.astype(jnp.bfloat16)] * lax.axis_size(DP)), DP, 0, 0),
+        axis=0,
+    )
     return (new_master, new_first, new_second, scaled_step, model_weights)
 
 

time: 167 us -> 110 us (0.66)
  waiting for transfers between devices: 96.8 us -> 0 us
  blocking collectives: 44.8 us -> 81.2 us
  other arithmetic: 1.93 us -> 17 us
  between operations: 16.1 us -> 2.69 us
    all_gather x1 -> x0, waiting for transfers between devices: 96.8 us -> none  [shards(): lax.all_gather(new_master.astype(jnp.bfloat16), DP, axis=0, tiled=True)]
    all_to_all x0 -> x1, blocking collectives: none -> 36.3 us  [shards(): lax.all_to_all(jnp.stack([new_master.astype(jnp.bfloat16)] * lax.axis_siz...]
    another operation x0 -> x1, other arithmetic: none -> 6.79 us  [shards(): jnp.stack([new_master.astype(jnp.bfloat16)] * lax.axis_size(DP))]
    all_to_all x0 -> x1, other arithmetic: none -> 6.15 us  [shards(): lax.all_to_all(jnp.stack([new_master.astype(jnp.bfloat16)] * lax.axis_siz...]
  transfers between devices with their start and end apart: 1 -> 0, of which waited for: 1 -> 0; matrix products, arithmetic and copies ran while one was open for 0% -> 0% of each run, Pallas kernels for 0% -> 0%
where the time goes in v1:
time: 110 us
  blocking collectives  81.2 us (74%)
  other arithmetic  17 us (15%)
  local copies, waits for them, and re-layouts  6.2 us (6%)
  between operations  2.69 us (2%)
  matrix products  2.58 us (2%)
    psum x4, blocking collectives, one_axis_at_a_time(): return functools.reduce(lax.psum, axes, value)  44.8 us
    all_to_all x1, blocking collectives, shards(): lax.all_to_all(jnp.stack([new_master.astype(jnp.bfloat16)] * lax.axis_siz...  36.3 us
    another operation x1, other arithmetic, shards(): jnp.stack([new_master.astype(jnp.bfloat16)] * lax.axis_size(DP))  6.79 us
    all_to_all x1, other arithmetic, shards(): lax.all_to_all(jnp.stack([new_master.astype(jnp.bfloat16)] * lax.axis_siz...  6.15 us
    unnamed x5, local copies, waits for them, and re-layouts  2.87 us

profile of v1, /device:TPU:1, one launch (start us, length us, event | category | flops | bytes accessed | tf_op | source)
XLA Modules:
  0.0 109.7 jit_solution(16383539031392459740)
XLA Ops:
  0.6 0.0 copy-start
  0.7 1.2 %slice.12 = s32[1]{0:T(128)} slice(s32[2048]{0:T(1024)} %param.16), slice={[0:1]} | slice | bytes 8 | tf_op jit(solution)/shard_map/slice | solution.py:94
  2.5 1.3 %broadcast_subtract_fusion = s32[2048]{0:T(1024)S(1)} fusion(s32[2048]{0:T(1024)} %param.16, s32[]{:T(128)} %bitcast.8), kind=kLoop, calls=%fused_computation.26 | loop fusion | flops 2048 | bytes 16388 | tf_op jit(solution)/shard_map/sub | solution.py:95
  4.5 0.7 convert_element_type.7
  5.9 0.1 fusion.10
  5.9 0.9 while.31
  6.0 0.5 fusion.23
  6.4 0.5 fusion.23
  6.9 1.4 %fusion.13 = (f32[2048]{0:T(1024)S(1)}, f32[2048]{0:T(1024)S(1)}, f32[2048]{0:T(1024)}, f32[2048]{0:T(1024)}, f32[2048]{0:T(1024)S(1)}) fusion(f32[2048]{0:T(1024)S(1)} %bitcast.56, f32[2048]{0:T(1024)} %param.12, f32[2048]{0:T(1024)} %param.13, f32[2048]{0:T(1024)} %param.14, f32[2048]{0:T(1024)} %param.15), kind=kLoop, calls=%fused_computation.34 | loop fusion | flops 30720 | bytes 81920 | tf_op jit(solution)/shard_map/mul | solution.py:102
  8.3 0.8 while.33
  8.3 0.4 convolution_add_fusion.2
  8.7 0.4 convolution_add_fusion.2
  9.2 0.3 dynamic_update_slice.10
  9.4 9.5 %psum.28 = f32[512,2]{0,1:T(2,128)S(1)} all-reduce(f32[512,2]{0,1:T(2,128)S(1)} %slice.16), channel_id=1, replica_groups=mesh['dp_0'=4,'dp_1'=8,'dp_2'=4,'dp_3'=2] {'dp_0'}, use_global_device_ids=true, to_apply=%region_4.5 | all-reduce | flops 1024 | bytes 8192 | tf_op jit(solution)/shard_map/psum | solution.py:20
  19.0 16.2 %psum.29 = f32[512,2]{0,1:T(2,128)S(1)} all-reduce(f32[512,2]{0,1:T(2,128)S(1)} %psum.28), channel_id=1, replica_groups=mesh['dp_0'=4,'dp_1'=8,'dp_2'=4,'dp_3'=2] {'dp_1'}, use_global_device_ids=true, to_apply=%region_5.6 | all-reduce | flops 1024 | bytes 8192 | tf_op jit(solution)/shard_map/psum | solution.py:20
  35.2 8.5 %psum.30 = f32[512,2]{0,1:T(2,128)S(1)} all-reduce(f32[512,2]{0,1:T(2,128)S(1)} %psum.29), channel_id=1, replica_groups=mesh['dp_0'=4,'dp_1'=8,'dp_2'=4,'dp_3'=2] {'dp_2'}, use_global_device_ids=true, to_apply=%region_6.7 | all-reduce | flops 1024 | bytes 8192 | tf_op jit(solution)/shard_map/psum | solution.py:20
  43.7 10.6 %psum.31 = f32[512,2]{0,1:T(2,128)S(1)} all-reduce(f32[512,2]{0,1:T(2,128)S(1)} %psum.30), channel_id=1, replica_groups=mesh['dp_0'=4,'dp_1'=8,'dp_2'=4,'dp_3'=2] {'dp_3'}, use_global_device_ids=true, to_apply=%region_7.8 | all-reduce | flops 1024 | bytes 8192 | tf_op jit(solution)/shard_map/psum | solution.py:20
  54.3 0.1 fusion.11
  54.4 0.9 while.32
  54.4 0.5 fusion.25
  54.9 0.5 fusion.25
  55.3 0.0 copy-done
  55.3 0.6 fusion.12
  56.0 1.1 stack.11
  57.1 0.5 broadcast.34
  57.6 6.8 %reduce.1 = bf16[256,2048]{1,0:T(8,128)(2,1)S(1)} reduce(bf16[256,1,2048]{2,1,0:T(2,128)(2,1)S(1)} %stack.11, bf16[]{:T(256)} %broadcast.34), dimensions={1}, to_apply=%stack.11.reduce_sub_computation | reduce | bytes 2097154 | tf_op jit(solution)/shard_map/stack | solution.py:110
  64.4 0.8 reshape.58
  65.2 36.3 %all_to_all.6 = bf16[256,2,1024]{2,1,0:T(2,128)(2,1)S(1)} all-to-all(bf16[256,2,1024]{2,1,0:T(2,128)(2,1)S(1)} %reshape.58), channel_id=1, replica_groups=mesh['dp_0'=4,'dp_1'=8,'dp_2'=4,'dp_3'=2] {'dp_0','dp_1','dp_2','dp_3'}, dimensions={0} | all-to-all | bytes 2097152 | tf_op jit(solution)/shard_map/all_to_all | solution.py:110
  101.5 0.9 reshape.59
  102.4 6.2 %reduce = bf16[256,2048]{1,0:T(8,128)(2,1)S(1)} reduce(bf16[256,1,2048]{2,1,0:T(2,128)(2,1)S(1)} %reshape.59, bf16[]{:T(256)} %constant.61), dimensions={1}, to_apply=%all_to_all.4.reduce_sub_computation | reduce | bytes 2097154 | tf_op jit(solution)/shard_map/all_to_all | solution.py:110
  108.5 1.2 %copy.11 = bf16[32,16,8,128]{3,1,2,0:T(8,128)(2,1)} copy(bf16[32,16,8,128]{3,2,1,0:T(8,128)(2,1)S(1)} %bitcast.51) | data formatting | bytes 2097152
  (16 shorter events, 0.2 us)
Async XLA Ops:
  0.6 54.7 %copy-start = (f32[2048]{0:T(1024)S(1)}, f32[2048]{0:T(1024)}, u32[]{:S(2)}) copy-start(f32[2048]{0:T(1024)} %param.12) | copy-start | bytes 24580
